TPU v7x, 128 devices: a whole 4x4x4 slice. The times are simulated.
128 devices in a mesh: gx: 8 (over y, core), gy: 16 (over x, z).
Axes of the slice: x: 4, y: 4, z: 4, core: 2. Of those that a mesh axis runs over, the one named last changes fastest.
Arguments:
- right_side: float32 [256, 512, 512], P('gx', 'gy'), as said below
- start_guess: float32 [256, 512, 512], P('gx', 'gy'), may hold values from -3 to 3
- conductivity: float32 [256, 512, 512], P('gx', 'gy'), may hold values from 0.5 to 8
Outputs:
- solution_field: float32 [256, 512, 512], P('gx', 'gy')
- estimate: float32 [], replicated
Inputs may be any that keep to these rules, and one draw needn't show every extreme that they name: `right_side`: A smoothly varying positive scale times noise, which may have a nonzero mean.
All inputs are finite; a program needn't handle non-finite values.
Results may differ from a plain program's by a relative error of at most 0.0003.
Values sent between devices are 32-bit elements; how exact they have to be, the bound alone decides.
A program may use at most 64 MiB of HBM per device.

v0:
```python
import jax
import jax.numpy as jnp
from jax import lax
from jax.sharding import Mesh
from jax.sharding import PartitionSpec as P

M = 3
GX_GY = ("gx_0", "gx_1", "gy_0", "gy_1")
GX = ("gx_0", "gx_1")
GY = ("gy_0", "gy_1")


def with_halo(x, sides, width):
    edges = {}
    for axis, dim in sides:
        devices, length = (lax.axis_size(axis), x.shape[dim])
        up = [(i, (i + 1) % devices) for i in range(devices - 1)]
        last = lax.slice_in_dim(x, length - width, length, axis=dim)
        initial = lax.slice_in_dim(x, 0, width, axis=dim)
        edges[dim] = (
            lax.ppermute(last, axis, up),
            lax.ppermute(initial, axis, [(b, a) for a, b in up]),
        )
    done = []
    for _, dim in sides:
        low, high = edges[dim]
        around = [(width, width) if d in done else (0, 0) for d in range(x.ndim)]
        x = jnp.concatenate([jnp.pad(low, around), x, jnp.pad(high, around)], axis=dim)
        done.append(dim)
    return x


def over_axes(x, axes):
    for axis in axes:
        x = lax.psum(x, axis)
    return x


def shifted(padded, which, sign):
    starts = [1, 1, 1]
    starts[which] = 1 + sign
    limits = [starts[dim] + padded.shape[dim] - 2 for dim in range(3)]
    return lax.slice(padded, starts, limits)


def extend_z(padded):
    return jnp.pad(padded, ((0, 0), (0, 0), (1, 1)))


def stencil(field, kappa_pad):
    padded = extend_z(with_halo(field, ((GX, 0), (GY, 1)), 1))
    centre = shifted(padded, 0, 0)
    middle = shifted(kappa_pad, 0, 0)
    result = jnp.zeros_like(centre)
    for which in range(3):
        for sign in (-1, 1):
            result = result + 0.5 * (middle + shifted(kappa_pad, which, sign)) * (
                centre - shifted(padded, which, sign)
            )
    return result


def global_norm(vector):
    return jnp.sqrt(over_axes(jnp.sum(vector * vector), GX_GY))


def least_squares(columns, beta):
    count = len(columns)
    rhs_vals = [beta] + [jnp.float32(0.0)] * count
    cosines = []
    sines = []
    upper = []
    for column in range(count):
        entries = list(columns[column])
        for earlier in range(column):
            first = entries[earlier]
            second = entries[earlier + 1]
            entries[earlier] = cosines[earlier] * first + sines[earlier] * second
            entries[earlier + 1] = -sines[earlier] * first + cosines[earlier] * second
        first = entries[column]
        second = entries[column + 1]
        radius = jnp.sqrt(first * first + second * second)
        cosines.append(first / radius)
        sines.append(second / radius)
        entries[column] = radius
        rhs_vals[column + 1] = -sines[column] * rhs_vals[column]
        rhs_vals[column] = cosines[column] * rhs_vals[column]
        upper.append(entries[: column + 1])
    coeffs = [None] * count
    for row in reversed(range(count)):
        value = rhs_vals[row]
        for later in range(row + 1, count):
            value = value - upper[later][row] * coeffs[later]
        coeffs[row] = value / upper[row][row]
    return (coeffs, jnp.abs(rhs_vals[count]))


def local(right_side, start_guess, conductivity):
    kappa_pad = extend_z(with_halo(conductivity, ((GX, 0), (GY, 1)), 1))
    start = right_side - stencil(start_guess, kappa_pad)
    beta = global_norm(start)
    basis = [start / beta]
    columns = []
    for column in range(M):
        vector = stencil(basis[column], kappa_pad)
        local_dots = jnp.stack([jnp.sum(vector * basis[earlier]) for earlier in range(column + 1)])
        coeff_all, squares = (
            over_axes(local_dots, GX_GY),
            over_axes(jnp.sum(vector * vector), GX_GY),
        )
        for earlier in range(column + 1):
            vector = vector - coeff_all[earlier] * basis[earlier]
        entries = [coeff_all[earlier] for earlier in range(column + 1)]
        length = jnp.sqrt(squares - jnp.sum(coeff_all * coeff_all))
        entries.append(length)
        columns.append(entries)
        basis.append(vector / length)
    coeffs, estimate = least_squares(columns, beta)
    solution_field = start_guess
    for column in range(M):
        solution_field = solution_field + coeffs[column] * basis[column]
    return (solution_field, estimate)


def solution(mesh):
    split = Mesh(mesh.devices.reshape(4, 2, 4, 4), ("gx_0", "gx_1", "gy_0", "gy_1"))
    return jax.shard_map(
        local,
        mesh=split,
        in_specs=(P(GX, GY, None), P(GX, GY, None), P(GX, GY, None)),
        out_specs=(P(GX, GY, None), P()),
        check_vma=False,
    )
```

profile of v0, /device:TPU:2, one launch (start us, length us, event | category | flops | bytes accessed | tf_op | source)
XLA Modules:
  0.0 298.1 jit_solution(9819572107874024284)
XLA Ops:
  5.9 3.8 %collective-permute-start.4 = (f32[32,1,512]{2,1,0:T(1,128)S(1)}, f32[32,1,512]{2,1,0:T(1,128)S(1)}, u32[]{:S(2)}, u32[]{:S(2)}) collective-permute-start(f32[32,1,512]{2,1,0:T(1,128)S(1)} %get-tuple-element.51), channel_id=1, source_target_pairs={{0,1},{1,2},{2,3},{3,4},{4,5},{5,6},{6,7},{7,8},{8,9},{9,10},{10,1... | collective-permute-start | bytes 196616 | tf_op jit(solution)/shard_map/ppermute | solution.py:21
  9.7 4.1 %collective-permute-start.6 = (f32[32,1,512]{2,1,0:T(1,128)S(1)}, f32[32,1,512]{2,1,0:T(1,128)S(1)}, u32[]{:S(2)}, u32[]{:S(2)}) collective-permute-start(f32[32,1,512]{2,1,0:T(1,128)S(1)} %get-tuple-element.52), channel_id=1, source_target_pairs={{1,0},{2,1},{3,2},{4,3},{5,4},{6,5},{7,6},{8,7},{9,8},{10,9},{11,1... | collective-permute-start | bytes 196616 | tf_op jit(solution)/shard_map/ppermute | solution.py:22
  14.7 4.0 %collective-permute-start.1 = (f32[1,32,512]{2,1,0:T(8,128)S(1)}, f32[1,32,512]{2,1,0:T(8,128)S(1)}, u32[]{:S(2)}, u32[]{:S(2)}) collective-permute-start(f32[1,32,512]{2,1,0:T(8,128)S(1)} %get-tuple-element.58), channel_id=1, source_target_pairs={{0,16},{16,32},{32,48},{48,64},{64,80},{80,96},{96,112},{1,17},{17... | collective-permute-start | bytes 196616 | tf_op jit(solution)/shard_map/ppermute | solution.py:21
  25.2 6.0 %collective-permute-start.7 = (f32[32,1,512]{2,1,0:T(1,128)S(1)}, f32[32,1,512]{2,1,0:T(1,128)S(1)}, u32[]{:S(2)}, u32[]{:S(2)}) collective-permute-start(f32[32,1,512]{2,1,0:T(1,128)S(1)} %get-tuple-element.56), channel_id=1, source_target_pairs={{1,0},{2,1},{3,2},{4,3},{5,4},{6,5},{7,6},{8,7},{9,8},{10,9},{11,1... | collective-permute-start | bytes 196616 | tf_op jit(solution)/shard_map/ppermute | solution.py:22
  35.8 8.7 %multiply_reduce_fusion.9 = (f32[]{:T(128)}, f32[32,32,512]{2,1,0:T(8,128)}) fusion(f32[32,32,512]{2,1,0:T(8,128)} %param.3, f32[32,32,512]{2,1,0:T(8,128)S(1)} %copy-done.11, f32[34,34,514]{2,1,0:T(8,128)S(1)} %select_maximum_fusion.12, f32[32,32,512]{2,1,0:T(8,128)S(1)} %copy-done.7, f32[34,34,514]{2,1,0:T(8,128)S(1)} %select_maximum_fusion.14, ...), kind=kLoop, calls=%fused_computation.144 | loop fusion | flops 20971520 | bytes 21774340 | tf_op jit(solution)/shard_map/reduce_sum | solution.py:64
  44.5 14.1 %psum.196 = f32[]{:T(128)} all-reduce(f32[]{:T(128)} %get-tuple-element.37), channel_id=1, replica_groups=mesh['gx_0'=4,'gx_1'=2,'gy_0'=4,'gy_1'=4] {'gx_0'}, use_global_device_ids=true, to_apply=%region_1.2 | all-reduce | flops 1 | bytes 8 | tf_op jit(solution)/shard_map/psum | solution.py:35
  61.7 9.2 %psum.198 = f32[]{:T(128)} all-reduce(f32[]{:T(128)} %psum.197), channel_id=1, replica_groups=mesh['gx_0'=4,'gx_1'=2,'gy_0'=4,'gy_1'=4] {'gy_0'}, use_global_device_ids=true, to_apply=%region_3.4 | all-reduce | flops 1 | bytes 8 | tf_op jit(solution)/shard_map/psum | solution.py:35
  70.9 11.8 %psum.199 = f32[]{:T(128)} all-reduce(f32[]{:T(128)} %psum.198), channel_id=1, replica_groups=mesh['gx_0'=4,'gx_1'=2,'gy_0'=4,'gy_1'=4] {'gy_1'}, use_global_device_ids=true, to_apply=%region_4.5 | all-reduce | flops 1 | bytes 8 | tf_op jit(solution)/shard_map/psum | solution.py:35
  87.3 6.0 %collective-permute-start.11 = (f32[32,1,512]{2,1,0:T(1,128)S(1)}, f32[32,1,512]{2,1,0:T(1,128)S(1)}, u32[]{:S(2)}, u32[]{:S(2)}) collective-permute-start(f32[32,1,512]{2,1,0:T(1,128)S(1)} %get-tuple-element.50), channel_id=1, source_target_pairs={{1,0},{2,1},{3,2},{4,3},{5,4},{6,5},{7,6},{8,7},{9,8},{10,9},{11,1... | collective-permute-start | bytes 196616 | tf_op jit(solution)/shard_map/ppermute | solution.py:22
  97.8 3.3 %select_maximum_fusion.8 = f32[34,34,514]{2,1,0:T(8,128)S(1)} fusion(f32[34,1,512]{2,1,0:T(1,128)S(1)} %pad.54, f32[34,1,512]{2,1,0:T(1,128)S(1)} %pad.53, f32[1,32,512]{2,1,0:T(8,128)S(1)} %collective-permute-done.9, f32[32,32,512]{2,1,0:T(8,128)S(1)} %broadcast_divide_fusion, f32[1,32,512]{2,1,0:T(8,128)S(1)} %collective-permute-done.8), kind=kLoop, calls=%fused_computation.10 | loop fusion | flops 7130208 | bytes 4744224 | tf_op jit(solution)/shard_map/concatenate | solution.py:28
  101.2 9.1 %multiply_reduce_fusion.8 = (f32[]{:T(128)}, f32[]{:T(128)}, f32[32,32,512]{2,1,0:T(8,128)}) fusion(f32[32,32,512]{2,1,0:T(8,128)S(1)} %broadcast_divide_fusion, f32[34,34,514]{2,1,0:T(8,128)S(1)} %select_maximum_fusion.8, f32[32,32,512]{2,1,0:T(8,128)S(1)} %copy-done.8, f32[34,34,514]{2,1,0:T(8,128)S(1)} %select_maximum_fusion.14, ...), kind=kLoop, calls=%fused_computation.143 | loop fusion | flops 23592960 | bytes 17448968 | tf_op jit(solution)/shard_map/reduce_sum | solution.py:106
  110.2 11.1 %all-reduce.23 = (f32[]{:T(128)}, f32[1]{0:T(128)}) all-reduce(f32[]{:T(128)} %get-tuple-element.10, f32[1]{0:T(128)} %bitcast), channel_id=1, replica_groups=mesh['gx_0'=4,'gx_1'=2,'gy_0'=4,'gy_1'=4] {'gx_0'}, use_global_device_ids=true, to_apply=%region_11.12 | all-reduce | flops 2 | bytes 16 | tf_op jit(solution)/shard_map/psum | solution.py:35
  121.3 3.1 %all-reduce.26 = (f32[]{:T(128)}, f32[1]{0:T(128)}) all-reduce(f32[]{:T(128)} %get-tuple-element.27, f32[1]{0:T(128)} %get-tuple-element.28), channel_id=1, replica_groups=mesh['gx_0'=4,'gx_1'=2,'gy_0'=4,'gy_1'=4] {'gx_1'}, use_global_device_ids=true, to_apply=%region_12.13 | all-reduce | flops 2 | bytes 16 | tf_op jit(solution)/shard_map/psum | solution.py:35
  124.4 7.8 %all-reduce.20 = (f32[]{:T(128)}, f32[1]{0:T(128)}) all-reduce(f32[]{:T(128)} %get-tuple-element.33, f32[1]{0:T(128)} %get-tuple-element.34), channel_id=1, replica_groups=mesh['gx_0'=4,'gx_1'=2,'gy_0'=4,'gy_1'=4] {'gy_0'}, use_global_device_ids=true, to_apply=%region_13.14 | all-reduce | flops 2 | bytes 16 | tf_op jit(solution)/shard_map/psum | solution.py:35
  132.2 9.5 %all-reduce.17 = (f32[]{:T(128)}, f32[1]{0:T(128)}) all-reduce(f32[]{:T(128)} %get-tuple-element.21, f32[1]{0:T(128)} %get-tuple-element.22), channel_id=1, replica_groups=mesh['gx_0'=4,'gx_1'=2,'gy_0'=4,'gy_1'=4] {'gy_1'}, use_global_device_ids=true, to_apply=%region_14.15 | all-reduce | flops 2 | bytes 16 | tf_op jit(solution)/shard_map/psum | solution.py:35
  143.7 3.4 %subtract_divide_fusion.1 = f32[32,32,512]{2,1,0:T(8,128)S(1)} fusion(f32[32,32,512]{2,1,0:T(8,128)} %get-tuple-element.36, f32[]{:T(128)S(6)} %sqrt.22, f32[]{:T(128)} %bitcast.1, f32[32,32,512]{2,1,0:T(8,128)} %get-tuple-element.38, f32[]{:T(128)S(6)} %sqrt.21), kind=kLoop, calls=%fused_computation.141 | loop fusion | flops 2097152 | bytes 6291468 | tf_op jit(solution)/shard_map/div | solution.py:117
  150.3 5.2 %collective-permute-start.15 = (f32[32,1,512]{2,1,0:T(1,128)S(1)}, f32[32,1,512]{2,1,0:T(1,128)S(1)}, u32[]{:S(2)}, u32[]{:S(2)}) collective-permute-start(f32[32,1,512]{2,1,0:T(1,128)S(1)} %get-tuple-element.46), channel_id=1, source_target_pairs={{1,0},{2,1},{3,2},{4,3},{5,4},{6,5},{7,6},{8,7},{9,8},{10,9},{11,1... | collective-permute-start | bytes 196616 | tf_op jit(solution)/shard_map/ppermute | solution.py:22
  158.2 3.2 %collective-permute-done.13 = f32[1,32,512]{2,1,0:T(8,128)S(1)} collective-permute-done((f32[1,32,512]{2,1,0:T(8,128)S(1)}, f32[1,32,512]{2,1,0:T(8,128)S(1)}, u32[]{:S(2)}, u32[]{:S(2)}) %collective-permute-start.13) | collective-permute-done | bytes 65568 | tf_op jit(solution)/shard_map/ppermute | solution.py:22
  161.4 3.3 %select_maximum_fusion.4 = f32[34,34,514]{2,1,0:T(8,128)S(1)} fusion(f32[34,1,512]{2,1,0:T(1,128)S(1)} %pad.57, f32[34,1,512]{2,1,0:T(1,128)S(1)} %pad.56, f32[1,32,512]{2,1,0:T(8,128)S(1)} %collective-permute-done.13, f32[32,32,512]{2,1,0:T(8,128)S(1)} %subtract_divide_fusion.1, f32[1,32,512]{2,1,0:T(8,128)S(1)} %collective-permute-done.12), kind=kLoop, calls=%fused_computation.6 | loop fusion | flops 7130208 | bytes 4744224 | tf_op jit(solution)/shard_map/concatenate | solution.py:28
  164.8 9.2 %multiply_reduce_fusion.6 = (f32[]{:T(128)}, f32[]{:T(128)}, f32[]{:T(128)}, f32[32,32,512]{2,1,0:T(8,128)}) fusion(f32[32,32,512]{2,1,0:T(8,128)S(1)} %subtract_divide_fusion.1, f32[34,34,514]{2,1,0:T(8,128)S(1)} %select_maximum_fusion.4, f32[32,32,512]{2,1,0:T(8,128)S(1)} %copy-done.9, f32[34,34,514]{2,1,0:T(8,128)S(1)} %select_maximum_fusion.14, ...), kind=kLoop, calls=%fused_computation.140 | loop fusion | flops 25165824 | bytes 19546128 | tf_op jit(solution)/shard_map/reduce_sum | solution.py:106
  175.4 11.2 %all-reduce.22 = (f32[]{:T(128)}, f32[2]{0:T(128)}) all-reduce(f32[]{:T(128)} %get-tuple-element.7, f32[2]{0:T(128)S(1)} %pad_maximum_fusion.32), channel_id=1, replica_groups=mesh['gx_0'=4,'gx_1'=2,'gy_0'=4,'gy_1'=4] {'gx_0'}, use_global_device_ids=true, to_apply=%region_22.23 | all-reduce | flops 3 | bytes 24 | tf_op jit(solution)/shard_map/psum | solution.py:35
  186.5 3.1 %all-reduce.25 = (f32[]{:T(128)}, f32[2]{0:T(128)S(1)}) all-reduce(f32[]{:T(128)} %get-tuple-element.25, f32[2]{0:T(128)} %get-tuple-element.26), channel_id=1, replica_groups=mesh['gx_0'=4,'gx_1'=2,'gy_0'=4,'gy_1'=4] {'gx_1'}, use_global_device_ids=true, to_apply=%region_23.24 | all-reduce | flops 3 | bytes 24 | tf_op jit(solution)/shard_map/psum | solution.py:35
  189.7 7.2 %all-reduce.19 = (f32[]{:T(128)}, f32[2]{0:T(128)}) all-reduce(f32[]{:T(128)} %get-tuple-element.31, f32[2]{0:T(128)S(1)} %get-tuple-element.32), channel_id=1, replica_groups=mesh['gx_0'=4,'gx_1'=2,'gy_0'=4,'gy_1'=4] {'gy_0'}, use_global_device_ids=true, to_apply=%region_24.25 | all-reduce | flops 3 | bytes 24 | tf_op jit(solution)/shard_map/psum | solution.py:35
  196.9 10.1 %all-reduce.16 = (f32[]{:T(128)}, f32[2]{0:T(128)S(1)}) all-reduce(f32[]{:T(128)} %get-tuple-element.19, f32[2]{0:T(128)} %get-tuple-element.20), channel_id=1, replica_groups=mesh['gx_0'=4,'gx_1'=2,'gy_0'=4,'gy_1'=4] {'gy_1'}, use_global_device_ids=true, to_apply=%region_25.26 | all-reduce | flops 3 | bytes 24 | tf_op jit(solution)/shard_map/psum | solution.py:35
  209.5 5.0 %subtract_divide_fusion = f32[32,32,512]{2,1,0:T(8,128)S(1)} fusion(f32[32,32,512]{2,1,0:T(8,128)} %copy-done.2, f32[32,32,512]{2,1,0:T(8,128)} %get-tuple-element.35, f32[]{:T(128)S(6)} %sqrt.24, f32[]{:T(128)} %bitcast.6, f32[]{:T(128)} %bitcast.5, f32[32,32,512]{2,1,0:T(8,128)} %get-tuple-element.38, f32[]{:T(128)S(6)} %sqrt.21), kind=kLoop, calls=%fused_computation.137 | loop fusion | flops 3145728 | bytes 8388624 | tf_op jit(solution)/shard_map/div | solution.py:117
  218.6 5.8 %collective-permute-start.19 = (f32[32,1,512]{2,1,0:T(1,128)}, f32[32,1,512]{2,1,0:T(1,128)}, u32[]{:S(2)}, u32[]{:S(2)}) collective-permute-start(f32[32,1,512]{2,1,0:T(1,128)} %get-tuple-element.42), channel_id=1, source_target_pairs={{1,0},{2,1},{3,2},{4,3},{5,4},{6,5},{7,6},{8,7},{9,8},{10,9},{11,1... | collective-permute-start | bytes 196616 | tf_op jit(solution)/shard_map/ppermute | solution.py:22
  234.3 4.8 %select_maximum_fusion = f32[34,34,514]{2,1,0:T(8,128)S(1)} fusion(f32[34,1,512]{2,1,0:T(1,128)S(1)} %pad.60, f32[34,1,512]{2,1,0:T(1,128)S(1)} %pad.59, f32[1,32,512]{2,1,0:T(8,128)} %collective-permute-done.17, f32[32,32,512]{2,1,0:T(8,128)} %copy-done.10, f32[1,32,512]{2,1,0:T(8,128)} %collective-permute-done.16), kind=kLoop, calls=%fused_computation.2 | loop fusion | flops 7130208 | bytes 4744224 | tf_op jit(solution)/shard_map/concatenate | solution.py:28
  239.2 11.1 %multiply_reduce_fusion = (f32[]{:T(128)}, f32[]{:T(128)}, f32[]{:T(128)}, f32[]{:T(128)}) fusion(f32[32,32,512]{2,1,0:T(8,128)} %copy-done.10, f32[32,32,512]{2,1,0:T(8,128)S(1)} %copy-done.3, f32[34,34,514]{2,1,0:T(8,128)S(1)} %select_maximum_fusion, f32[32,32,512]{2,1,0:T(8,128)} %param.5, f32[34,34,514]{2,1,0:T(8,128)S(1)} %select_maximum_fusion.14, ...), kind=kLoop, calls=%fused_computation.133 | loop fusion | flops 26214400 | bytes 19546132 | tf_op jit(solution)/shard_map/reduce_sum | solution.py:109
  252.1 10.5 %all-reduce.21 = (f32[3]{0:T(128)S(1)}, f32[]{:T(128)}) all-reduce(f32[3]{0:T(128)S(1)} %pad_maximum_fusion.33, f32[]{:T(128)} %get-tuple-element.2), channel_id=1, replica_groups=mesh['gx_0'=4,'gx_1'=2,'gy_0'=4,'gy_1'=4] {'gx_0'}, use_global_device_ids=true, to_apply=%region_30.31 | all-reduce | flops 4 | bytes 32 | tf_op jit(solution)/shard_map/psum | solution.py:35
  265.7 8.0 %all-reduce.18 = (f32[3]{0:T(128)S(1)}, f32[]{:T(128)}) all-reduce(f32[3]{0:T(128)S(1)} %get-tuple-element.29, f32[]{:T(128)} %get-tuple-element.30), channel_id=1, replica_groups=mesh['gx_0'=4,'gx_1'=2,'gy_0'=4,'gy_1'=4] {'gy_0'}, use_global_device_ids=true, to_apply=%region_32.33 | all-reduce | flops 4 | bytes 32 | tf_op jit(solution)/shard_map/psum | solution.py:35
  273.7 10.7 %all-reduce.15 = (f32[3]{0:T(128)S(1)}, f32[]{:T(128)}) all-reduce(f32[3]{0:T(128)S(1)} %get-tuple-element.17, f32[]{:T(128)} %get-tuple-element.18), channel_id=1, replica_groups=mesh['gx_0'=4,'gx_1'=2,'gy_0'=4,'gy_1'=4] {'gy_1'}, use_global_device_ids=true, to_apply=%region_33.34 | all-reduce | flops 4 | bytes 32 | tf_op jit(solution)/shard_map/psum | solution.py:35
  291.0 6.0 %multiply_add_fusion = f32[32,32,512]{2,1,0:T(8,128)} fusion(f32[32,32,512]{2,1,0:T(8,128)} %copy-done.10, f32[32,32,512]{2,1,0:T(8,128)} %copy-done.2, f32[32,32,512]{2,1,0:T(8,128)} %param.4, f32[]{:T(128)S(6)} %div.56, f32[]{:T(128)S(6)} %div.57, f32[]{:T(128)S(6)} %div.58, f32[32,32,512]{2,1,0:T(8,128)} %get-tuple-element.38, f32[]{:T(128)S(6)} %sqrt.21), kind=kLoop, calls=%fused_computation.132 | loop fusion | flops 3670016 | bytes 10485776 | tf_op jit(solution)/shard_map/add | solution.py:121
  (117 shorter events, 52.0 us)
Async XLA Ops:
  1.5 18.6 %collective-permute-start = (f32[1,32,512]{2,1,0:T(8,128)S(1)}, f32[1,32,512]{2,1,0:T(8,128)S(1)}, u32[]{:S(2)}, u32[]{:S(2)}) collective-permute-start(f32[1,32,512]{2,1,0:T(8,128)S(1)} %get-tuple-element.54), channel_id=1, source_target_pairs={{0,16},{16,32},{32,48},{48,64},{64,80},{80,96},{96,112},{1,17},{17... | collective-permute-start | bytes 196616 | tf_op jit(solution)/shard_map/ppermute | solution.py:21
  3.3 28.0 %collective-permute-start.2 = (f32[1,32,512]{2,1,0:T(8,128)S(1)}, f32[1,32,512]{2,1,0:T(8,128)S(1)}, u32[]{:S(2)}, u32[]{:S(2)}) collective-permute-start(f32[1,32,512]{2,1,0:T(8,128)S(1)} %get-tuple-element.53), channel_id=1, source_target_pairs={{16,0},{32,16},{48,32},{64,48},{80,64},{96,80},{112,96},{17,1},{33... | collective-permute-start | bytes 196616 | tf_op jit(solution)/shard_map/ppermute | solution.py:22
  5.9 17.3 %collective-permute-start.4 = (f32[32,1,512]{2,1,0:T(1,128)S(1)}, f32[32,1,512]{2,1,0:T(1,128)S(1)}, u32[]{:S(2)}, u32[]{:S(2)}) collective-permute-start(f32[32,1,512]{2,1,0:T(1,128)S(1)} %get-tuple-element.51), channel_id=1, source_target_pairs={{0,1},{1,2},{2,3},{3,4},{4,5},{5,6},{6,7},{7,8},{8,9},{9,10},{10,1... | collective-permute-start | bytes 196616 | tf_op jit(solution)/shard_map/ppermute | solution.py:21
  9.7 15.5 %collective-permute-start.6 = (f32[32,1,512]{2,1,0:T(1,128)S(1)}, f32[32,1,512]{2,1,0:T(1,128)S(1)}, u32[]{:S(2)}, u32[]{:S(2)}) collective-permute-start(f32[32,1,512]{2,1,0:T(1,128)S(1)} %get-tuple-element.52), channel_id=1, source_target_pairs={{1,0},{2,1},{3,2},{4,3},{5,4},{6,5},{7,6},{8,7},{9,8},{10,9},{11,1... | collective-permute-start | bytes 196616 | tf_op jit(solution)/shard_map/ppermute | solution.py:22
  14.7 18.2 %collective-permute-start.1 = (f32[1,32,512]{2,1,0:T(8,128)S(1)}, f32[1,32,512]{2,1,0:T(8,128)S(1)}, u32[]{:S(2)}, u32[]{:S(2)}) collective-permute-start(f32[1,32,512]{2,1,0:T(8,128)S(1)} %get-tuple-element.58), channel_id=1, source_target_pairs={{0,16},{16,32},{32,48},{48,64},{64,80},{80,96},{96,112},{1,17},{17... | collective-permute-start | bytes 196616 | tf_op jit(solution)/shard_map/ppermute | solution.py:21
  20.1 15.6 %copy-start.16 = (f32[1,32,512]{2,1,0:T(8,128)}, f32[1,32,512]{2,1,0:T(8,128)S(1)}, u32[]{:S(2)}) copy-start(f32[1,32,512]{2,1,0:T(8,128)S(1)} %collective-permute-done) | copy-start | bytes 196612
  20.1 14.0 %collective-permute-start.3 = (f32[1,32,512]{2,1,0:T(8,128)S(1)}, f32[1,32,512]{2,1,0:T(8,128)S(1)}, u32[]{:S(2)}, u32[]{:S(2)}) collective-permute-start(f32[1,32,512]{2,1,0:T(8,128)S(1)} %get-tuple-element.57), channel_id=1, source_target_pairs={{16,0},{32,16},{48,32},{64,48},{80,64},{96,80},{112,96},{17,1},{33... | collective-permute-start | bytes 196616 | tf_op jit(solution)/shard_map/ppermute | solution.py:22
  23.2 10.7 %collective-permute-start.5 = (f32[32,1,512]{2,1,0:T(1,128)S(1)}, f32[32,1,512]{2,1,0:T(1,128)S(1)}, u32[]{:S(2)}, u32[]{:S(2)}) collective-permute-start(f32[32,1,512]{2,1,0:T(1,128)S(1)} %get-tuple-element.55), channel_id=1, source_target_pairs={{0,1},{1,2},{2,3},{3,4},{4,5},{5,6},{6,7},{7,8},{8,9},{9,10},{10,1... | collective-permute-start | bytes 196616 | tf_op jit(solution)/shard_map/ppermute | solution.py:21
  25.2 8.8 %collective-permute-start.7 = (f32[32,1,512]{2,1,0:T(1,128)S(1)}, f32[32,1,512]{2,1,0:T(1,128)S(1)}, u32[]{:S(2)}, u32[]{:S(2)}) collective-permute-start(f32[32,1,512]{2,1,0:T(1,128)S(1)} %get-tuple-element.56), channel_id=1, source_target_pairs={{1,0},{2,1},{3,2},{4,3},{5,4},{6,5},{7,6},{8,7},{9,8},{10,9},{11,1... | collective-permute-start | bytes 196616 | tf_op jit(solution)/shard_map/ppermute | solution.py:22
  85.4 10.6 %collective-permute-start.10 = (f32[32,1,512]{2,1,0:T(1,128)S(1)}, f32[32,1,512]{2,1,0:T(1,128)S(1)}, u32[]{:S(2)}, u32[]{:S(2)}) collective-permute-start(f32[32,1,512]{2,1,0:T(1,128)S(1)} %get-tuple-element.49), channel_id=1, source_target_pairs={{0,1},{1,2},{2,3},{3,4},{4,5},{5,6},{6,7},{7,8},{8,9},{9,10},{10,1... | collective-permute-start | bytes 196616 | tf_op jit(solution)/shard_map/ppermute | solution.py:21
  87.3 8.7 %collective-permute-start.11 = (f32[32,1,512]{2,1,0:T(1,128)S(1)}, f32[32,1,512]{2,1,0:T(1,128)S(1)}, u32[]{:S(2)}, u32[]{:S(2)}) collective-permute-start(f32[32,1,512]{2,1,0:T(1,128)S(1)} %get-tuple-element.50), channel_id=1, source_target_pairs={{1,0},{2,1},{3,2},{4,3},{5,4},{6,5},{7,6},{8,7},{9,8},{10,9},{11,1... | collective-permute-start | bytes 196616 | tf_op jit(solution)/shard_map/ppermute | solution.py:22
  93.4 2.8 collective-permute-start.8
  94.7 3.1 %collective-permute-start.9 = (f32[1,32,512]{2,1,0:T(8,128)S(1)}, f32[1,32,512]{2,1,0:T(8,128)S(1)}, u32[]{:S(2)}, u32[]{:S(2)}) collective-permute-start(f32[1,32,512]{2,1,0:T(8,128)S(1)} %get-tuple-element.48), channel_id=1, source_target_pairs={{16,0},{32,16},{48,32},{64,48},{80,64},{96,80},{112,96},{17,1},{33... | collective-permute-start | bytes 196616 | tf_op jit(solution)/shard_map/ppermute | solution.py:22
  96.1 5.0 %copy-start.5 = (f32[34,32,512]{2,1,0:T(8,128)S(1)}, f32[34,32,512]{2,1,0:T(8,128)}, u32[]{:S(2)}) copy-start(f32[34,32,512]{2,1,0:T(8,128)} %copy-done.4) | copy-start | bytes 6684676
  96.1 5.0 %copy-start.8 = (f32[32,32,512]{2,1,0:T(8,128)S(1)}, f32[32,32,512]{2,1,0:T(8,128)}, u32[]{:S(2)}) copy-start(f32[32,32,512]{2,1,0:T(8,128)} %param.5) | copy-start | bytes 6291460
  96.1 5.0 %copy-start.13 = (f32[34,1,512]{2,1,0:T(1,128)S(1)}, f32[34,1,512]{2,1,0:T(1,128)}, u32[]{:S(2)}) copy-start(f32[34,1,512]{2,1,0:T(1,128)} %copy-done.12) | copy-start | bytes 208900
  96.1 5.0 %copy-start.17 = (f32[1,32,512]{2,1,0:T(8,128)S(1)}, f32[1,32,512]{2,1,0:T(8,128)}, u32[]{:S(2)}) copy-start(f32[1,32,512]{2,1,0:T(8,128)} %copy-done.16) | copy-start | bytes 196612
  147.1 17.7 %copy-start.2 = (f32[32,32,512]{2,1,0:T(8,128)}, f32[32,32,512]{2,1,0:T(8,128)S(1)}, u32[]{:S(2)}) copy-start(f32[32,32,512]{2,1,0:T(8,128)S(1)} %subtract_divide_fusion.1) | copy-start | bytes 6291460
  147.1 17.7 %copy-start.9 = (f32[32,32,512]{2,1,0:T(8,128)S(1)}, f32[32,32,512]{2,1,0:T(8,128)}, u32[]{:S(2)}) copy-start(f32[32,32,512]{2,1,0:T(8,128)} %param.5) | copy-start | bytes 6291460
  147.2 10.8 %collective-permute-start.14 = (f32[32,1,512]{2,1,0:T(1,128)S(1)}, f32[32,1,512]{2,1,0:T(1,128)S(1)}, u32[]{:S(2)}, u32[]{:S(2)}) collective-permute-start(f32[32,1,512]{2,1,0:T(1,128)S(1)} %get-tuple-element.45), channel_id=1, source_target_pairs={{0,1},{1,2},{2,3},{3,4},{4,5},{5,6},{6,7},{7,8},{8,9},{9,10},{10,1... | collective-permute-start | bytes 196616 | tf_op jit(solution)/shard_map/ppermute | solution.py:21
  150.3 7.8 %collective-permute-start.15 = (f32[32,1,512]{2,1,0:T(1,128)S(1)}, f32[32,1,512]{2,1,0:T(1,128)S(1)}, u32[]{:S(2)}, u32[]{:S(2)}) collective-permute-start(f32[32,1,512]{2,1,0:T(1,128)S(1)} %get-tuple-element.46), channel_id=1, source_target_pairs={{1,0},{2,1},{3,2},{4,3},{5,4},{6,5},{7,6},{8,7},{9,8},{10,9},{11,1... | collective-permute-start | bytes 196616 | tf_op jit(solution)/shard_map/ppermute | solution.py:22
  155.4 2.8 collective-permute-start.12
  156.7 4.7 %collective-permute-start.13 = (f32[1,32,512]{2,1,0:T(8,128)S(1)}, f32[1,32,512]{2,1,0:T(8,128)S(1)}, u32[]{:S(2)}, u32[]{:S(2)}) collective-permute-start(f32[1,32,512]{2,1,0:T(8,128)S(1)} %get-tuple-element.44), channel_id=1, source_target_pairs={{16,0},{32,16},{48,32},{64,48},{80,64},{96,80},{112,96},{17,1},{33... | collective-permute-start | bytes 196616 | tf_op jit(solution)/shard_map/ppermute | solution.py:22
  158.2 6.6 %copy-start = (f32[32,32,512]{2,1,0:T(8,128)S(1)}, f32[32,32,512]{2,1,0:T(8,128)}, u32[]{:S(2)}) copy-start(f32[32,32,512]{2,1,0:T(8,128)} %get-tuple-element.38) | copy-start | bytes 6291460
  158.2 6.6 %copy-start.6 = (f32[34,32,512]{2,1,0:T(8,128)S(1)}, f32[34,32,512]{2,1,0:T(8,128)}, u32[]{:S(2)}) copy-start(f32[34,32,512]{2,1,0:T(8,128)} %copy-done.4) | copy-start | bytes 6684676
  158.2 6.6 %copy-start.14 = (f32[34,1,512]{2,1,0:T(1,128)S(1)}, f32[34,1,512]{2,1,0:T(1,128)}, u32[]{:S(2)}) copy-start(f32[34,1,512]{2,1,0:T(1,128)} %copy-done.12) | copy-start | bytes 208900
  158.2 6.6 %copy-start.18 = (f32[1,32,512]{2,1,0:T(8,128)S(1)}, f32[1,32,512]{2,1,0:T(8,128)}, u32[]{:S(2)}) copy-start(f32[1,32,512]{2,1,0:T(8,128)} %copy-done.16) | copy-start | bytes 196612
  158.2 6.6 %copy-start.22 = (f32[1,32,512]{2,1,0:T(8,128)S(1)}, f32[1,32,512]{2,1,0:T(8,128)}, u32[]{:S(2)}) copy-start(f32[1,32,512]{2,1,0:T(8,128)} %copy-done.20) | copy-start | bytes 196612
  216.5 15.9 %collective-permute-start.18 = (f32[32,1,512]{2,1,0:T(1,128)}, f32[32,1,512]{2,1,0:T(1,128)}, u32[]{:S(2)}, u32[]{:S(2)}) collective-permute-start(f32[32,1,512]{2,1,0:T(1,128)} %get-tuple-element.41), channel_id=1, source_target_pairs={{0,1},{1,2},{2,3},{3,4},{4,5},{5,6},{6,7},{7,8},{8,9},{9,10},{10,1... | collective-permute-start | bytes 196616 | tf_op jit(solution)/shard_map/ppermute | solution.py:21
  218.6 14.7 %collective-permute-start.19 = (f32[32,1,512]{2,1,0:T(1,128)}, f32[32,1,512]{2,1,0:T(1,128)}, u32[]{:S(2)}, u32[]{:S(2)}) collective-permute-start(f32[32,1,512]{2,1,0:T(1,128)} %get-tuple-element.42), channel_id=1, source_target_pairs={{1,0},{2,1},{3,2},{4,3},{5,4},{6,5},{7,6},{8,7},{9,8},{10,9},{11,1... | collective-permute-start | bytes 196616 | tf_op jit(solution)/shard_map/ppermute | solution.py:22
  224.4 9.8 %collective-permute-start.16 = (f32[1,32,512]{2,1,0:T(8,128)}, f32[1,32,512]{2,1,0:T(8,128)}, u32[]{:S(2)}, u32[]{:S(2)}) collective-permute-start(f32[1,32,512]{2,1,0:T(8,128)} %get-tuple-element.39), channel_id=1, source_target_pairs={{0,16},{16,32},{32,48},{48,64},{64,80},{80,96},{96,112},{1,17},{17... | collective-permute-start | bytes 196616 | tf_op jit(solution)/shard_map/ppermute | solution.py:21
  226.3 7.9 %collective-permute-start.17 = (f32[1,32,512]{2,1,0:T(8,128)}, f32[1,32,512]{2,1,0:T(8,128)}, u32[]{:S(2)}, u32[]{:S(2)}) collective-permute-start(f32[1,32,512]{2,1,0:T(8,128)} %get-tuple-element.40), channel_id=1, source_target_pairs={{16,0},{32,16},{48,32},{64,48},{80,64},{96,80},{112,96},{17,1},{33... | collective-permute-start | bytes 196616 | tf_op jit(solution)/shard_map/ppermute | solution.py:22
  (12 other events, 48.2 us)
where the time goes:
time: 300 us; the launch traced here: 298 us
  blocking collectives  134 us (45%)
  other arithmetic  73.3 us (24%)
  starting transfers between devices  56.7 us (19%)
  between operations  16.6 us (6%)
  local copies, waits for them, and re-layouts  13 us (4%)
  waiting for transfers between devices  4.88 us (2%)
    psum x16, blocking collectives, over_axes(): x = lax.psum(x, axis)  134 us
    ppermute x10, starting transfers between devices, with_halo(): lax.ppermute(initial, axis, [(b, a) for a, b in up])  33.6 us
    ppermute x10, starting transfers between devices, with_halo(): lax.ppermute(last, axis, up)  23.1 us
    reduce_sum x2, other arithmetic, local(): jnp.sum(vector * basis[earlier])  18.3 us
    concatenate x5, other arithmetic, with_halo(): jnp.concatenate([jnp.pad(low, around), x, jnp.pad(high, around)], axis=dim)  14.6 us
    reduce_sum x1, other arithmetic, local(): jnp.sum(vector * vector)  11.1 us
    reduce_sum x1, other arithmetic, global_norm(): return jnp.sqrt(over_axes(jnp.sum(vector * vector), GX_GY))  8.7 us
    div x2, other arithmetic, local(): basis.append(vector / length)  8.35 us
  transfers between devices with their start and end apart: 20, of which 2 were waited for; matrix products, arithmetic and copies ran while one was open for 3% of the time, Pallas kernels for 0%

commit v1 on v0

--- a/solution.py
+++ b/solution.py
@@ -32,7 +32,7 @@
 
 def over_axes(x, axes):
     for axis in axes:
-        x = lax.psum(x, axis)
+        x = jnp.sum(lax.all_gather(x, axis), axis=0)
     return x
 
 

time: 300 us -> 382 us (1.27)
  local copies, waits for them, and re-layouts: 13 us -> 72.2 us
  other arithmetic: 73.3 us -> 96.2 us
  blocking collectives: 134 us -> 130 us
  between operations: 16.6 us -> 20.5 us
    psum x16 -> x0, blocking collectives: 134 us -> none  [over_axes(): x = lax.psum(x, axis)]
    unnamed x0 -> x16, blocking collectives: none -> 130 us
    unnamed x52 -> x126, local copies, waits for them, and re-layouts: 3.33 us -> 57.4 us
    reduce_sum x0 -> x28, other arithmetic: none -> 21.9 us  [over_axes(): x = jnp.sum(lax.all_gather(x, axis), axis=0)]
where the time goes in v1:
time: 382 us; the launch traced here: 380 us
  blocking collectives  130 us (34%)
  other arithmetic  96.2 us (25%)
  local copies, waits for them, and re-layouts  72.2 us (19%)
  starting transfers between devices  57.5 us (15%)
  between operations  20.5 us (5%)
    unnamed x16, blocking collectives  130 us
    unnamed x126, local copies, waits for them, and re-layouts  57.4 us
    ppermute x10, starting transfers between devices, with_halo(): lax.ppermute(initial, axis, [(b, a) for a, b in up])  33.7 us
    ppermute x10, starting transfers between devices, with_halo(): lax.ppermute(last, axis, up)  23.7 us
    reduce_sum x28, other arithmetic, over_axes(): x = jnp.sum(lax.all_gather(x, axis), axis=0)  21.9 us
    reduce_sum x2, other arithmetic, local(): jnp.sum(vector * basis[earlier])  18.1 us
    concatenate x5, other arithmetic, with_halo(): jnp.concatenate([jnp.pad(low, around), x, jnp.pad(high, around)], axis=dim)  14.6 us
    reduce_sum x1, other arithmetic, local(): jnp.sum(vector * vector)  11.3 us
  transfers between devices with their start and end apart: 20, of which 2 were waited for; matrix products, arithmetic and copies ran while one was open for 3% of the time, Pallas kernels for 0%

profile of v1, /device:TPU:2, one launch (start us, length us, event | category | flops | bytes accessed | tf_op | source)
XLA Modules:
  0.0 379.5 jit_solution(14269148524854147913)
XLA Ops:
  5.9 3.8 %collective-permute-start.4 = (f32[32,1,512]{2,1,0:T(1,128)S(1)}, f32[32,1,512]{2,1,0:T(1,128)S(1)}, u32[]{:S(2)}, u32[]{:S(2)}) collective-permute-start(f32[32,1,512]{2,1,0:T(1,128)S(1)} %get-tuple-element.51), channel_id=1, source_target_pairs={{0,1},{1,2},{2,3},{3,4},{4,5},{5,6},{6,7},{7,8},{8,9},{9,10},{10,1... | collective-permute-start | bytes 196616 | tf_op jit(solution)/shard_map/ppermute | solution.py:21
  9.7 4.1 %collective-permute-start.6 = (f32[32,1,512]{2,1,0:T(1,128)S(1)}, f32[32,1,512]{2,1,0:T(1,128)S(1)}, u32[]{:S(2)}, u32[]{:S(2)}) collective-permute-start(f32[32,1,512]{2,1,0:T(1,128)S(1)} %get-tuple-element.52), channel_id=1, source_target_pairs={{1,0},{2,1},{3,2},{4,3},{5,4},{6,5},{7,6},{8,7},{9,8},{10,9},{11,1... | collective-permute-start | bytes 196616 | tf_op jit(solution)/shard_map/ppermute | solution.py:22
  15.4 4.6 %collective-permute-start.1 = (f32[1,32,512]{2,1,0:T(8,128)}, f32[1,32,512]{2,1,0:T(8,128)}, u32[]{:S(2)}, u32[]{:S(2)}) collective-permute-start(f32[1,32,512]{2,1,0:T(8,128)} %get-tuple-element.58), channel_id=1, source_target_pairs={{0,16},{16,32},{32,48},{48,64},{64,80},{80,96},{96,112},{1,17},{17... | collective-permute-start | bytes 196616 | tf_op jit(solution)/shard_map/ppermute | solution.py:21
  28.4 6.0 %collective-permute-start.7 = (f32[32,1,512]{2,1,0:T(1,128)}, f32[32,1,512]{2,1,0:T(1,128)S(1)}, u32[]{:S(2)}, u32[]{:S(2)}) collective-permute-start(f32[32,1,512]{2,1,0:T(1,128)} %get-tuple-element.56), channel_id=1, source_target_pairs={{1,0},{2,1},{3,2},{4,3},{5,4},{6,5},{7,6},{8,7},{9,8},{10,9},{11,1... | collective-permute-start | bytes 196616 | tf_op jit(solution)/shard_map/ppermute | solution.py:22
  39.1 8.7 %multiply_reduce_fusion.9 = (f32[]{:T(128)}, f32[32,32,512]{2,1,0:T(8,128)}) fusion(f32[32,32,512]{2,1,0:T(8,128)} %param.3, f32[32,32,512]{2,1,0:T(8,128)S(1)} %copy-done.11, f32[34,34,514]{2,1,0:T(8,128)S(1)} %select_maximum_fusion.12, f32[32,32,512]{2,1,0:T(8,128)S(1)} %copy-done.7, f32[34,34,514]{2,1,0:T(8,128)S(1)} %select_maximum_fusion.14, ...), kind=kLoop, calls=%fused_computation.144 | loop fusion | flops 20971520 | bytes 21774340 | tf_op jit(solution)/shard_map/reduce_sum | solution.py:64
  52.1 13.5 %all-reduce.15 = f32[4]{0:T(128)} all-reduce(f32[4]{0:T(128)} %dynamic-update-slice), channel_id=1, replica_groups=mesh['gx_0'=4,'gx_1'=2,'gy_0'=4,'gy_1'=4] {'gx_0'}, use_global_device_ids=true, to_apply=%add.15 | all-reduce | flops 4 | bytes 32
  71.3 3.1 all-reduce.16
  79.3 8.7 %all-reduce.17 = f32[4]{0:T(128)S(1)} all-reduce(f32[4]{0:T(128)} %dynamic-update-slice.2), channel_id=1, replica_groups=mesh['gx_0'=4,'gx_1'=2,'gy_0'=4,'gy_1'=4] {'gy_0'}, use_global_device_ids=true, to_apply=%add.17 | all-reduce | flops 4 | bytes 32
  89.9 11.8 %all-reduce.18 = f32[4]{0:T(128)} all-reduce(f32[4]{0:T(128)S(1)} %dynamic-update-slice.3), channel_id=1, replica_groups=mesh['gx_0'=4,'gx_1'=2,'gy_0'=4,'gy_1'=4] {'gy_1'}, use_global_device_ids=true, to_apply=%add.18 | all-reduce | flops 4 | bytes 32
  107.6 6.0 %collective-permute-start.11 = (f32[32,1,512]{2,1,0:T(1,128)S(1)}, f32[32,1,512]{2,1,0:T(1,128)S(1)}, u32[]{:S(2)}, u32[]{:S(2)}) collective-permute-start(f32[32,1,512]{2,1,0:T(1,128)S(1)} %get-tuple-element.50), channel_id=1, source_target_pairs={{1,0},{2,1},{3,2},{4,3},{5,4},{6,5},{7,6},{8,7},{9,8},{10,9},{11,1... | collective-permute-start | bytes 196616 | tf_op jit(solution)/shard_map/ppermute | solution.py:22
  118.1 3.3 select_maximum_fusion.8
  121.4 8.8 %multiply_reduce_fusion.8 = (f32[]{:T(128)}, f32[]{:T(128)}, f32[32,32,512]{2,1,0:T(8,128)}) fusion(f32[32,32,512]{2,1,0:T(8,128)S(1)} %broadcast_divide_fusion, f32[34,34,514]{2,1,0:T(8,128)S(1)} %select_maximum_fusion.8, f32[32,32,512]{2,1,0:T(8,128)S(1)} %copy-done.8, f32[34,34,514]{2,1,0:T(8,128)S(1)} %select_maximum_fusion.14, ...), kind=kLoop, calls=%fused_computation.143 | loop fusion | flops 23592960 | bytes 17448968 | tf_op jit(solution)/shard_map/reduce_sum | solution.py:106
  134.8 11.1 %all-reduce.51 = (f32[4]{0:T(128)S(1)}, f32[4]{0:T(128)}) all-reduce(f32[4]{0:T(128)} %dynamic-update-slice.8, f32[4]{0:T(128)} %copy-done.27), channel_id=1, replica_groups=mesh['gx_0'=4,'gx_1'=2,'gy_0'=4,'gy_1'=4] {'gx_0'}, use_global_device_ids=true, to_apply=%add.23 | all-reduce | flops 8 | bytes 64
  153.8 3.1 all-reduce.54
  164.8 7.8 %all-reduce.48 = (f32[4]{0:T(128)S(1)}, f32[4]{0:T(128)}) all-reduce(f32[4]{0:T(128)} %dynamic-update-slice.10, f32[4]{0:T(128)} %dynamic-update-slice.6), channel_id=1, replica_groups=mesh['gx_0'=4,'gx_1'=2,'gy_0'=4,'gy_1'=4] {'gy_0'}, use_global_device_ids=true, to_apply=%add.25 | all-reduce | flops 8 | bytes 64
  180.2 9.5 %all-reduce.45 = (f32[4]{0:T(128)S(1)}, f32[4]{0:T(128)}) all-reduce(f32[4]{0:T(128)} %dynamic-update-slice.11, f32[4]{0:T(128)} %dynamic-update-slice.7), channel_id=1, replica_groups=mesh['gx_0'=4,'gx_1'=2,'gy_0'=4,'gy_1'=4] {'gy_1'}, use_global_device_ids=true, to_apply=%add.26 | all-reduce | flops 8 | bytes 64
  193.7 3.4 subtract_divide_fusion.1
  200.3 5.2 %collective-permute-start.15 = (f32[32,1,512]{2,1,0:T(1,128)S(1)}, f32[32,1,512]{2,1,0:T(1,128)S(1)}, u32[]{:S(2)}, u32[]{:S(2)}) collective-permute-start(f32[32,1,512]{2,1,0:T(1,128)S(1)} %get-tuple-element.46), channel_id=1, source_target_pairs={{1,0},{2,1},{3,2},{4,3},{5,4},{6,5},{7,6},{8,7},{9,8},{10,9},{11,1... | collective-permute-start | bytes 196616 | tf_op jit(solution)/shard_map/ppermute | solution.py:22
  211.5 3.3 select_maximum_fusion.4
  214.8 9.3 %multiply_reduce_fusion.6 = (f32[]{:T(128)}, f32[]{:T(128)}, f32[]{:T(128)}, f32[32,32,512]{2,1,0:T(8,128)}) fusion(f32[32,32,512]{2,1,0:T(8,128)S(1)} %subtract_divide_fusion.1, f32[34,34,514]{2,1,0:T(8,128)S(1)} %select_maximum_fusion.4, f32[32,32,512]{2,1,0:T(8,128)S(1)} %copy-done.9, f32[34,34,514]{2,1,0:T(8,128)S(1)} %select_maximum_fusion.14, ...), kind=kLoop, calls=%fused_computation.140 | loop fusion | flops 25165824 | bytes 19546128 | tf_op jit(solution)/shard_map/reduce_sum | solution.py:106
  228.2 11.4 %all-reduce.50 = (f32[4]{0:T(128)}, f32[8]{0:T(128)}) all-reduce(f32[4]{0:T(128)} %copy-done.28, f32[8]{0:T(128)S(1)} %maximum_dynamic-update-slice_fusion), channel_id=1, replica_groups=mesh['gx_0'=4,'gx_1'=2,'gy_0'=4,'gy_1'=4] {'gx_0'}, use_global_device_ids=true, to_apply=%add.31 | all-reduce | flops 12 | bytes 96
  245.0 3.2 all-reduce.53
  253.7 7.2 %all-reduce.47 = (f32[4]{0:T(128)}, f32[8]{0:T(128)}) all-reduce(f32[4]{0:T(128)} %copy-done.30, f32[8]{0:T(128)S(1)} %dynamic-update-slice.14), channel_id=1, replica_groups=mesh['gx_0'=4,'gx_1'=2,'gy_0'=4,'gy_1'=4] {'gy_0'}, use_global_device_ids=true, to_apply=%add.33 | all-reduce | flops 12 | bytes 96
  266.1 10.4 %all-reduce.44 = (f32[4]{0:T(128)}, f32[8]{0:T(128)}) all-reduce(f32[4]{0:T(128)} %copy-done.31, f32[8]{0:T(128)S(1)} %dynamic-update-slice.15), channel_id=1, replica_groups=mesh['gx_0'=4,'gx_1'=2,'gy_0'=4,'gy_1'=4] {'gy_1'}, use_global_device_ids=true, to_apply=%add.34 | all-reduce | flops 12 | bytes 96
  282.8 5.0 %subtract_divide_fusion = f32[32,32,512]{2,1,0:T(8,128)S(1)} fusion(f32[32,32,512]{2,1,0:T(8,128)} %copy-done.2, f32[32,32,512]{2,1,0:T(8,128)} %get-tuple-element.35, f32[]{:T(128)S(6)} %sqrt.24, f32[]{:T(128)} %bitcast.23, f32[]{:T(128)} %bitcast.22, f32[32,32,512]{2,1,0:T(8,128)} %get-tuple-element.38, f32[]{:T(128)S(6)} %sqrt.21), kind=kLoop, calls=%fused_computation.137 | loop fusion | flops 3145728 | bytes 8388624 | tf_op jit(solution)/shard_map/div | solution.py:117
  292.0 5.8 %collective-permute-start.19 = (f32[32,1,512]{2,1,0:T(1,128)}, f32[32,1,512]{2,1,0:T(1,128)}, u32[]{:S(2)}, u32[]{:S(2)}) collective-permute-start(f32[32,1,512]{2,1,0:T(1,128)} %get-tuple-element.42), channel_id=1, source_target_pairs={{1,0},{2,1},{3,2},{4,3},{5,4},{6,5},{7,6},{8,7},{9,8},{10,9},{11,1... | collective-permute-start | bytes 196616 | tf_op jit(solution)/shard_map/ppermute | solution.py:22
  308.9 4.8 %select_maximum_fusion = f32[34,34,514]{2,1,0:T(8,128)S(1)} fusion(f32[34,1,512]{2,1,0:T(1,128)S(1)} %pad.60, f32[34,1,512]{2,1,0:T(1,128)S(1)} %pad.59, f32[1,32,512]{2,1,0:T(8,128)} %collective-permute-done.17, f32[32,32,512]{2,1,0:T(8,128)} %copy-done.10, f32[1,32,512]{2,1,0:T(8,128)} %collective-permute-done.16), kind=kLoop, calls=%fused_computation.2 | loop fusion | flops 7130208 | bytes 4744224 | tf_op jit(solution)/shard_map/concatenate | solution.py:28
  313.8 11.3 %multiply_reduce_fusion = (f32[]{:T(128)}, f32[]{:T(128)}, f32[]{:T(128)}, f32[]{:T(128)}) fusion(f32[32,32,512]{2,1,0:T(8,128)} %copy-done.10, f32[32,32,512]{2,1,0:T(8,128)S(1)} %copy-done.3, f32[34,34,514]{2,1,0:T(8,128)S(1)} %select_maximum_fusion, f32[32,32,512]{2,1,0:T(8,128)} %param.5, f32[34,34,514]{2,1,0:T(8,128)S(1)} %select_maximum_fusion.14, ...), kind=kLoop, calls=%fused_computation.133 | loop fusion | flops 26214400 | bytes 19546132 | tf_op jit(solution)/shard_map/reduce_sum | solution.py:109
  328.5 9.8 %all-reduce.49 = (f32[12]{0:T(128)S(1)}, f32[4]{0:T(128)S(1)}) all-reduce(f32[12]{0:T(128)S(1)} %maximum_dynamic-update-slice_fusion.1, f32[4]{0:T(128)S(1)} %dynamic-update-slice.24), channel_id=6, replica_groups=mesh['gx_0'=4,'gx_1'=2,'gy_0'=4,'gy_1'=4] {'gx_0'}, use_global_device_ids=true, to_apply=%add.35 | all-reduce | flops 16 | bytes 128
  345.5 7.4 %all-reduce.46 = (f32[12]{0:T(128)S(1)}, f32[4]{0:T(128)S(1)}) all-reduce(f32[12]{0:T(128)S(1)} %dynamic-update-slice.22, f32[4]{0:T(128)S(1)} %dynamic-update-slice.26), channel_id=8, replica_groups=mesh['gx_0'=4,'gx_1'=2,'gy_0'=4,'gy_1'=4] {'gy_0'}, use_global_device_ids=true, to_apply=%add.37 | all-reduce | flops 16 | bytes 128
  355.1 10.0 %all-reduce.43 = (f32[12]{0:T(128)S(1)}, f32[4]{0:T(128)S(1)}) all-reduce(f32[12]{0:T(128)S(1)} %dynamic-update-slice.23, f32[4]{0:T(128)S(1)} %dynamic-update-slice.27), channel_id=9, replica_groups=mesh['gx_0'=4,'gx_1'=2,'gy_0'=4,'gy_1'=4] {'gy_1'}, use_global_device_ids=true, to_apply=%add.38 | all-reduce | flops 16 | bytes 128
  372.4 6.0 %multiply_add_fusion = f32[32,32,512]{2,1,0:T(8,128)} fusion(f32[32,32,512]{2,1,0:T(8,128)} %copy-done.10, f32[32,32,512]{2,1,0:T(8,128)} %copy-done.2, f32[32,32,512]{2,1,0:T(8,128)} %param.4, f32[]{:T(128)S(6)} %div.56, f32[]{:T(128)S(6)} %div.57, f32[]{:T(128)S(6)} %div.58, f32[32,32,512]{2,1,0:T(8,128)} %get-tuple-element.38, f32[]{:T(128)S(6)} %sqrt.21), kind=kLoop, calls=%fused_computation.132 | loop fusion | flops 3670016 | bytes 10485776 | tf_op jit(solution)/shard_map/add | solution.py:121
  (227 shorter events, 131.6 us)
Async XLA Ops:
  1.5 21.8 %collective-permute-start = (f32[1,32,512]{2,1,0:T(8,128)S(1)}, f32[1,32,512]{2,1,0:T(8,128)S(1)}, u32[]{:S(2)}, u32[]{:S(2)}) collective-permute-start(f32[1,32,512]{2,1,0:T(8,128)S(1)} %get-tuple-element.54), channel_id=1, source_target_pairs={{0,16},{16,32},{32,48},{48,64},{64,80},{80,96},{96,112},{1,17},{17... | collective-permute-start | bytes 196616 | tf_op jit(solution)/shard_map/ppermute | solution.py:21
  3.3 25.1 %collective-permute-start.2 = (f32[1,32,512]{2,1,0:T(8,128)S(1)}, f32[1,32,512]{2,1,0:T(8,128)S(1)}, u32[]{:S(2)}, u32[]{:S(2)}) collective-permute-start(f32[1,32,512]{2,1,0:T(8,128)S(1)} %get-tuple-element.53), channel_id=1, source_target_pairs={{16,0},{32,16},{48,32},{64,48},{80,64},{96,80},{112,96},{17,1},{33... | collective-permute-start | bytes 196616 | tf_op jit(solution)/shard_map/ppermute | solution.py:22
  5.9 20.5 %collective-permute-start.4 = (f32[32,1,512]{2,1,0:T(1,128)S(1)}, f32[32,1,512]{2,1,0:T(1,128)S(1)}, u32[]{:S(2)}, u32[]{:S(2)}) collective-permute-start(f32[32,1,512]{2,1,0:T(1,128)S(1)} %get-tuple-element.51), channel_id=1, source_target_pairs={{0,1},{1,2},{2,3},{3,4},{4,5},{5,6},{6,7},{7,8},{8,9},{9,10},{10,1... | collective-permute-start | bytes 196616 | tf_op jit(solution)/shard_map/ppermute | solution.py:21
  9.7 24.7 %collective-permute-start.6 = (f32[32,1,512]{2,1,0:T(1,128)S(1)}, f32[32,1,512]{2,1,0:T(1,128)S(1)}, u32[]{:S(2)}, u32[]{:S(2)}) collective-permute-start(f32[32,1,512]{2,1,0:T(1,128)S(1)} %get-tuple-element.52), channel_id=1, source_target_pairs={{1,0},{2,1},{3,2},{4,3},{5,4},{6,5},{7,6},{8,7},{9,8},{10,9},{11,1... | collective-permute-start | bytes 196616 | tf_op jit(solution)/shard_map/ppermute | solution.py:22
  15.4 20.8 %collective-permute-start.1 = (f32[1,32,512]{2,1,0:T(8,128)}, f32[1,32,512]{2,1,0:T(8,128)}, u32[]{:S(2)}, u32[]{:S(2)}) collective-permute-start(f32[1,32,512]{2,1,0:T(8,128)} %get-tuple-element.58), channel_id=1, source_target_pairs={{0,16},{16,32},{32,48},{48,64},{64,80},{80,96},{96,112},{1,17},{17... | collective-permute-start | bytes 196616 | tf_op jit(solution)/shard_map/ppermute | solution.py:21
  23.3 14.0 %collective-permute-start.3 = (f32[1,32,512]{2,1,0:T(8,128)}, f32[1,32,512]{2,1,0:T(8,128)S(1)}, u32[]{:S(2)}, u32[]{:S(2)}) collective-permute-start(f32[1,32,512]{2,1,0:T(8,128)} %get-tuple-element.57), channel_id=1, source_target_pairs={{16,0},{32,16},{48,32},{64,48},{80,64},{96,80},{112,96},{17,1},{33... | collective-permute-start | bytes 196616 | tf_op jit(solution)/shard_map/ppermute | solution.py:22
  26.4 10.8 %collective-permute-start.5 = (f32[32,1,512]{2,1,0:T(1,128)}, f32[32,1,512]{2,1,0:T(1,128)S(1)}, u32[]{:S(2)}, u32[]{:S(2)}) collective-permute-start(f32[32,1,512]{2,1,0:T(1,128)} %get-tuple-element.55), channel_id=1, source_target_pairs={{0,1},{1,2},{2,3},{3,4},{4,5},{5,6},{6,7},{7,8},{8,9},{9,10},{10,1... | collective-permute-start | bytes 196616 | tf_op jit(solution)/shard_map/ppermute | solution.py:21
  28.4 6.1 %copy-start.21 = (f32[1,32,512]{2,1,0:T(8,128)}, f32[1,32,512]{2,1,0:T(8,128)S(1)}, u32[]{:S(2)}) copy-start(f32[1,32,512]{2,1,0:T(8,128)S(1)} %collective-permute-done.2) | copy-start | bytes 196612
  28.4 8.9 %collective-permute-start.7 = (f32[32,1,512]{2,1,0:T(1,128)}, f32[32,1,512]{2,1,0:T(1,128)S(1)}, u32[]{:S(2)}, u32[]{:S(2)}) collective-permute-start(f32[32,1,512]{2,1,0:T(1,128)} %get-tuple-element.56), channel_id=1, source_target_pairs={{1,0},{2,1},{3,2},{4,3},{5,4},{6,5},{7,6},{8,7},{9,8},{10,9},{11,1... | collective-permute-start | bytes 196616 | tf_op jit(solution)/shard_map/ppermute | solution.py:22
  39.0 39.7 %copy-start.26 = (u32[128]{0:T(128)S(1)}, u32[128]{0:T(128)}, u32[]{:S(2)}) copy-start(u32[128]{0:T(128)} %constant.53) | copy-start | bytes 1540
  105.7 10.8 %collective-permute-start.10 = (f32[32,1,512]{2,1,0:T(1,128)S(1)}, f32[32,1,512]{2,1,0:T(1,128)S(1)}, u32[]{:S(2)}, u32[]{:S(2)}) collective-permute-start(f32[32,1,512]{2,1,0:T(1,128)S(1)} %get-tuple-element.49), channel_id=1, source_target_pairs={{0,1},{1,2},{2,3},{3,4},{4,5},{5,6},{6,7},{7,8},{8,9},{9,10},{10,1... | collective-permute-start | bytes 196616 | tf_op jit(solution)/shard_map/ppermute | solution.py:21
  107.6 8.9 %collective-permute-start.11 = (f32[32,1,512]{2,1,0:T(1,128)S(1)}, f32[32,1,512]{2,1,0:T(1,128)S(1)}, u32[]{:S(2)}, u32[]{:S(2)}) collective-permute-start(f32[32,1,512]{2,1,0:T(1,128)S(1)} %get-tuple-element.50), channel_id=1, source_target_pairs={{1,0},{2,1},{3,2},{4,3},{5,4},{6,5},{7,6},{8,7},{9,8},{10,9},{11,1... | collective-permute-start | bytes 196616 | tf_op jit(solution)/shard_map/ppermute | solution.py:22
  113.6 3.0 collective-permute-start.8
  114.9 3.1 collective-permute-start.9
  116.5 4.8 %copy-start.5 = (f32[34,32,512]{2,1,0:T(8,128)S(1)}, f32[34,32,512]{2,1,0:T(8,128)}, u32[]{:S(2)}) copy-start(f32[34,32,512]{2,1,0:T(8,128)} %copy-done.4) | copy-start | bytes 6684676
  116.6 4.8 %copy-start.8 = (f32[32,32,512]{2,1,0:T(8,128)S(1)}, f32[32,32,512]{2,1,0:T(8,128)}, u32[]{:S(2)}) copy-start(f32[32,32,512]{2,1,0:T(8,128)} %param.5) | copy-start | bytes 6291460
  116.6 4.8 %copy-start.13 = (f32[34,1,512]{2,1,0:T(1,128)S(1)}, f32[34,1,512]{2,1,0:T(1,128)}, u32[]{:S(2)}) copy-start(f32[34,1,512]{2,1,0:T(1,128)} %copy-done.12) | copy-start | bytes 208900
  197.1 17.7 %copy-start.2 = (f32[32,32,512]{2,1,0:T(8,128)}, f32[32,32,512]{2,1,0:T(8,128)S(1)}, u32[]{:S(2)}) copy-start(f32[32,32,512]{2,1,0:T(8,128)S(1)} %subtract_divide_fusion.1) | copy-start | bytes 6291460
  197.1 17.7 %copy-start.9 = (f32[32,32,512]{2,1,0:T(8,128)S(1)}, f32[32,32,512]{2,1,0:T(8,128)}, u32[]{:S(2)}) copy-start(f32[32,32,512]{2,1,0:T(8,128)} %param.5) | copy-start | bytes 6291460
  197.2 12.8 %collective-permute-start.14 = (f32[32,1,512]{2,1,0:T(1,128)S(1)}, f32[32,1,512]{2,1,0:T(1,128)S(1)}, u32[]{:S(2)}, u32[]{:S(2)}) collective-permute-start(f32[32,1,512]{2,1,0:T(1,128)S(1)} %get-tuple-element.45), channel_id=1, source_target_pairs={{0,1},{1,2},{2,3},{3,4},{4,5},{5,6},{6,7},{7,8},{8,9},{9,10},{10,1... | collective-permute-start | bytes 196616 | tf_op jit(solution)/shard_map/ppermute | solution.py:21
  200.3 9.8 %collective-permute-start.15 = (f32[32,1,512]{2,1,0:T(1,128)S(1)}, f32[32,1,512]{2,1,0:T(1,128)S(1)}, u32[]{:S(2)}, u32[]{:S(2)}) collective-permute-start(f32[32,1,512]{2,1,0:T(1,128)S(1)} %get-tuple-element.46), channel_id=1, source_target_pairs={{1,0},{2,1},{3,2},{4,3},{5,4},{6,5},{7,6},{8,7},{9,8},{10,9},{11,1... | collective-permute-start | bytes 196616 | tf_op jit(solution)/shard_map/ppermute | solution.py:22
  205.5 4.8 %collective-permute-start.12 = (f32[1,32,512]{2,1,0:T(8,128)S(1)}, f32[1,32,512]{2,1,0:T(8,128)S(1)}, u32[]{:S(2)}, u32[]{:S(2)}) collective-permute-start(f32[1,32,512]{2,1,0:T(8,128)S(1)} %get-tuple-element.43), channel_id=1, source_target_pairs={{0,16},{16,32},{32,48},{48,64},{64,80},{80,96},{96,112},{1,17},{17... | collective-permute-start | bytes 196616 | tf_op jit(solution)/shard_map/ppermute | solution.py:21
  206.8 4.7 %collective-permute-start.13 = (f32[1,32,512]{2,1,0:T(8,128)S(1)}, f32[1,32,512]{2,1,0:T(8,128)S(1)}, u32[]{:S(2)}, u32[]{:S(2)}) collective-permute-start(f32[1,32,512]{2,1,0:T(8,128)S(1)} %get-tuple-element.44), channel_id=1, source_target_pairs={{16,0},{32,16},{48,32},{64,48},{80,64},{96,80},{112,96},{17,1},{33... | collective-permute-start | bytes 196616 | tf_op jit(solution)/shard_map/ppermute | solution.py:22
  289.8 17.2 %collective-permute-start.18 = (f32[32,1,512]{2,1,0:T(1,128)}, f32[32,1,512]{2,1,0:T(1,128)}, u32[]{:S(2)}, u32[]{:S(2)}) collective-permute-start(f32[32,1,512]{2,1,0:T(1,128)} %get-tuple-element.41), channel_id=1, source_target_pairs={{0,1},{1,2},{2,3},{3,4},{4,5},{5,6},{6,7},{7,8},{8,9},{9,10},{10,1... | collective-permute-start | bytes 196616 | tf_op jit(solution)/shard_map/ppermute | solution.py:21
  292.0 15.9 %collective-permute-start.19 = (f32[32,1,512]{2,1,0:T(1,128)}, f32[32,1,512]{2,1,0:T(1,128)}, u32[]{:S(2)}, u32[]{:S(2)}) collective-permute-start(f32[32,1,512]{2,1,0:T(1,128)} %get-tuple-element.42), channel_id=1, source_target_pairs={{1,0},{2,1},{3,2},{4,3},{5,4},{6,5},{7,6},{8,7},{9,8},{10,9},{11,1... | collective-permute-start | bytes 196616 | tf_op jit(solution)/shard_map/ppermute | solution.py:22
  297.8 11.1 %collective-permute-start.16 = (f32[1,32,512]{2,1,0:T(8,128)}, f32[1,32,512]{2,1,0:T(8,128)}, u32[]{:S(2)}, u32[]{:S(2)}) collective-permute-start(f32[1,32,512]{2,1,0:T(8,128)} %get-tuple-element.39), channel_id=1, source_target_pairs={{0,16},{16,32},{32,48},{48,64},{64,80},{80,96},{96,112},{1,17},{17... | collective-permute-start | bytes 196616 | tf_op jit(solution)/shard_map/ppermute | solution.py:21
  299.7 9.2 %collective-permute-start.17 = (f32[1,32,512]{2,1,0:T(8,128)}, f32[1,32,512]{2,1,0:T(8,128)}, u32[]{:S(2)}, u32[]{:S(2)}) collective-permute-start(f32[1,32,512]{2,1,0:T(8,128)} %get-tuple-element.40), channel_id=1, source_target_pairs={{16,0},{32,16},{48,32},{64,48},{80,64},{96,80},{112,96},{17,1},{33... | collective-permute-start | bytes 196616 | tf_op jit(solution)/shard_map/ppermute | solution.py:22
  308.8 4.9 %copy-start.1 = (f32[32,32,512]{2,1,0:T(8,128)S(1)}, f32[32,32,512]{2,1,0:T(8,128)}, u32[]{:S(2)}) copy-start(f32[32,32,512]{2,1,0:T(8,128)} %get-tuple-element.38) | copy-start | bytes 6291460
  308.8 4.9 %copy-start.3 = (f32[32,32,512]{2,1,0:T(8,128)S(1)}, f32[32,32,512]{2,1,0:T(8,128)}, u32[]{:S(2)}) copy-start(f32[32,32,512]{2,1,0:T(8,128)} %copy-done.2) | copy-start | bytes 6291460
  308.8 4.9 %copy-start.15 = (f32[34,1,512]{2,1,0:T(1,128)S(1)}, f32[34,1,512]{2,1,0:T(1,128)}, u32[]{:S(2)}) copy-start(f32[34,1,512]{2,1,0:T(1,128)} %copy-done.12) | copy-start | bytes 208900
  308.8 4.9 %copy-start.20 = (f32[1,32,512]{2,1,0:T(8,128)S(1)}, f32[1,32,512]{2,1,0:T(8,128)}, u32[]{:S(2)}) copy-start(f32[1,32,512]{2,1,0:T(8,128)} %copy-done.16) | copy-start | bytes 196612
  308.9 4.9 %copy-start.25 = (f32[1,32,512]{2,1,0:T(8,128)S(1)}, f32[1,32,512]{2,1,0:T(8,128)}, u32[]{:S(2)}) copy-start(f32[1,32,512]{2,1,0:T(8,128)} %copy-done.21) | copy-start | bytes 196612
  (20 other events, 56.3 us)
